TPU v7x, 32 devices: a whole 2x2x4 slice. The times are simulated.
32 devices in a mesh: row: 4 (over y, core), col: 8 (over z, x).
Axes of the slice: x: 2, y: 2, z: 4, core: 2. Of those that a mesh axis runs over, the one named last changes fastest.
Arguments:
- volume: float32 [8, 1024, 1024], P(None, 'row', 'col'), may hold values from -6 to 6
- ray_weights: float32 [16, 1024], P(None, 'row'), may hold values from 0.5 to 2
- shear_weights: bfloat16 [16, 128, 128], replicated, may hold values from -0.5 to 0.5
- shear_offsets: int32 [16], replicated, may hold values from 0 to 7
- measured: float32 [16, 8, 1024], P('row', None, 'col'), may hold values from -6 to 6
Outputs:
- residual: float32 [16, 8, 1024], P('row', None, 'col')
- gradient: float32 [8, 1024, 1024], P(None, 'row', 'col')
All inputs are finite; a program needn't handle non-finite values.
Results may differ from a plain program's by a relative error of at most 0.0003.
Values sent between devices are 32-bit elements; how exact they have to be, the bound alone decides.
A program may use at most 64 MiB of HBM per device.

v0:
```python
import math

import jax
import jax.numpy as jnp
from jax import lax
from jax.sharding import PartitionSpec as P


def from_behind(value, axis, steps):
    count = lax.axis_size(axis)
    pairs = [(source, (source + steps) % count) for source in range(count)]
    return lax.ppermute(value, axis, pairs)


def push_cols(values, amounts):
    total_bits = lax.axis_size("col").bit_length() - 1
    current = values
    for level in range(total_bits):
        moved = from_behind(current, "col", 1 << level)
        chosen = jnp.bitwise_and(jnp.right_shift(amounts, level), 1) == 1
        current = jnp.where(chosen[:, None, None], moved, current)
    return current


def pull_cols(values, amounts):
    total_bits = lax.axis_size("col").bit_length() - 1
    current = values
    for level in range(total_bits):
        moved = from_behind(current, "col", -(1 << level))
        chosen = jnp.bitwise_and(jnp.right_shift(amounts, level), 1) == 1
        current = jnp.where(chosen[:, None, None], moved, current)
    return current


def on_device(volume, ray_weights, shear_weights, shear_offsets, measured):
    highest = lax.Precision.HIGHEST
    row_count = lax.axis_size("row")
    col_count = lax.axis_size("col")
    row_index = lax.axis_index("row")
    slab_rows = volume.shape[1]
    per_owner = measured.shape[0]
    factor = 1.0 / math.sqrt(slab_rows * row_count)
    shear = shear_weights.astype(jnp.float32)
    offsets_owned = lax.dynamic_slice_in_dim(shear_offsets, row_index * per_owner, per_owner, 0)
    tilesum = jnp.einsum("ax,sxy->asy", ray_weights, volume, precision=highest) * factor
    outgoing = jnp.einsum("asy,ayz->asz", tilesum, shear, precision=highest)
    received = lax.all_to_all(outgoing, "row", split_axis=0, concat_axis=0, tiled=True)
    sources = jnp.arange(received.shape[0], dtype=jnp.int32) // per_owner
    amounts = jnp.tile(offsets_owned, row_count) * sources % col_count
    landed = push_cols(received, amounts)
    projection = jnp.sum(landed.reshape((row_count, per_owner) + landed.shape[1:]), axis=0)
    residual = projection - measured
    copies = jnp.tile(residual, (row_count, 1, 1))
    shifted = pull_cols(copies, amounts)
    arrived = lax.all_to_all(shifted, "row", split_axis=0, concat_axis=0, tiled=True)
    spread = jnp.einsum("asz,ayz->asy", arrived, shear, precision=highest)
    gradient = jnp.einsum("ax,asy->sxy", ray_weights, spread, precision=highest) * factor
    return (residual, gradient)


def solution(mesh):
    placed = (P(None, "row", "col"), P(None, "row"), P(), P(), P("row", None, "col"))
    return jax.shard_map(
        on_device,
        mesh=mesh,
        in_specs=placed,
        out_specs=(P("row", None, "col"), P(None, "row", "col")),
        check_vma=False,
    )
```

profile of v0, /device:TPU:0, one launch (start us, length us, event | category | flops | bytes accessed | tf_op | source)
XLA Modules:
  0.0 56.8 jit_solution(5039697128480997424)
XLA Ops:
  0.6 0.0 copy-start
  0.7 1.2 %copy-done = f32[8,256,128]{2,1,0:T(8,128)S(1)} copy-done((f32[8,256,128]{2,1,0:T(8,128)S(1)}, f32[8,256,128]{2,1,0:T(8,128)}, u32[]{:S(2)}) %copy-start) | copy-done | bytes 1048600
  1.9 1.3 %fusion.5 = f32[16,8,128]{2,0,1:T(8,128)S(1)} fusion(f32[8,256,128]{2,1,0:T(8,128)S(1)} %copy-done, f32[16,256]{1,0:T(8,128)} %param.6), kind=kOutput, calls=%fused_computation.13 | convolution fusion | flops 50331648 | bytes 1130496 | tf_op jit(solution)/shard_map/ax,sxy->asy/dot_general | solution.py:45
  3.2 1.2 %fusion.2 = f32[16,8,128]{2,1,0:T(8,128)} fusion(bf16[16,128,128]{2,1,0:T(8,128)(2,1)S(1)} %copy-done.1, f32[16,8,128]{2,0,1:T(8,128)S(1)} %fusion.5), kind=kOutput, calls=%fused_computation.4 | convolution fusion | flops 25182208 | bytes 655360 | tf_op jit(solution)/shard_map/asy,ayz->asz/dot_general | solution.py:46
  4.3 4.3 %all-to-all-start = ((f32[16,8,128]{2,1,0:T(8,128)}), f32[16,8,128]{2,1,0:T(8,128)S(1)}, u32[]{:S(2)}, u32[]{:S(2)}) async-start(f32[16,8,128]{2,1,0:T(8,128)} %fusion.2), calls=%async_computation | async-start | bytes 131072 | tf_op jit(solution)/shard_map/all_to_all | solution.py:47
  8.6 0.7 %copy-done.5 = s32[16]{0:T(128)S(1)} copy-done((s32[16]{0:T(128)S(1)}, s32[16]{0:T(128)}, u32[]{:S(2)}) %copy-start.5) | copy-done | bytes 88
  9.3 0.1 dynamic_slice.3
  9.3 0.1 tile.9
  9.5 3.3 %all-to-all-done = f32[16,8,128]{2,1,0:T(8,128)S(1)} async-done(((f32[16,8,128]{2,1,0:T(8,128)}), f32[16,8,128]{2,1,0:T(8,128)S(1)}, u32[]{:S(2)}, u32[]{:S(2)}) %all-to-all-start) | async-done | bytes 65568 | tf_op jit(solution)/shard_map/all_to_all | solution.py:47
  12.7 2.0 %collective-permute-start = (f32[16,8,128]{2,1,0:T(8,128)S(1)}, f32[16,8,128]{2,1,0:T(8,128)S(1)}, u32[]{:S(2)}, u32[]{:S(2)}) collective-permute-start(f32[16,8,128]{2,1,0:T(8,128)S(1)} %all-to-all-done), channel_id=1, source_target_pairs={{0,1},{1,2},{2,3},{3,4},{4,5},{5,6},{6,7},{7,0},{8,9},{9,10},{10,1... | collective-permute-start | bytes 196616 | tf_op jit(solution)/shard_map/ppermute | solution.py:12
  14.7 5.3 %collective-permute-done = f32[16,8,128]{2,1,0:T(8,128)S(1)} collective-permute-done((f32[16,8,128]{2,1,0:T(8,128)S(1)}, f32[16,8,128]{2,1,0:T(8,128)S(1)}, u32[]{:S(2)}, u32[]{:S(2)}) %collective-permute-start) | collective-permute-done | bytes 65568 | tf_op jit(solution)/shard_map/ppermute | solution.py:12
  20.0 0.1 broadcast_select_fusion
  20.1 0.1 collective-permute-start.1
  20.1 6.7 %collective-permute-done.1 = f32[16,8,128]{2,1,0:T(8,128)S(1)} collective-permute-done((f32[16,8,128]{2,1,0:T(8,128)S(1)}, f32[16,8,128]{2,1,0:T(8,128)S(1)}, u32[]{:S(2)}, u32[]{:S(2)}) %collective-permute-start.1) | collective-permute-done | bytes 65568 | tf_op jit(solution)/shard_map/ppermute | solution.py:12
  26.8 0.1 broadcast_select_fusion.2
  26.9 0.1 collective-permute-start.2
  27.0 5.2 %collective-permute-done.2 = f32[16,8,128]{2,1,0:T(8,128)S(1)} collective-permute-done((f32[16,8,128]{2,1,0:T(8,128)S(1)}, f32[16,8,128]{2,1,0:T(8,128)S(1)}, u32[]{:S(2)}, u32[]{:S(2)}) %collective-permute-start.2) | collective-permute-done | bytes 65568 | tf_op jit(solution)/shard_map/ppermute | solution.py:12
  32.1 0.1 broadcast_select_fusion.4
  32.2 0.7 %copy-done.4 = f32[4,8,128]{2,1,0:T(8,128)S(1)} copy-done((f32[4,8,128]{2,1,0:T(8,128)S(1)}, f32[4,8,128]{2,1,0:T(8,128)}, u32[]{:S(2)}) %copy-start.4) | copy-done | bytes 16408
  32.9 0.3 collective-permute-start.3
  33.2 4.1 %collective-permute-done.3 = f32[16,8,128]{2,1,0:T(8,128)S(1)} collective-permute-done((f32[16,8,128]{2,1,0:T(8,128)S(1)}, f32[16,8,128]{2,1,0:T(8,128)S(1)}, u32[]{:S(2)}, u32[]{:S(2)}) %collective-permute-start.3) | collective-permute-done | bytes 65568 | tf_op jit(solution)/shard_map/ppermute | solution.py:12
  37.3 0.1 bitcast_select_fusion
  37.3 0.1 collective-permute-start.4
  37.4 4.3 %collective-permute-done.4 = f32[16,8,128]{2,1,0:T(8,128)S(1)} collective-permute-done((f32[16,8,128]{2,1,0:T(8,128)S(1)}, f32[16,8,128]{2,1,0:T(8,128)S(1)}, u32[]{:S(2)}, u32[]{:S(2)}) %collective-permute-start.4) | collective-permute-done | bytes 65568 | tf_op jit(solution)/shard_map/ppermute | solution.py:12
  41.7 0.1 broadcast_select_fusion.1
  41.8 0.1 collective-permute-start.5
  41.8 5.2 %collective-permute-done.5 = f32[16,8,128]{2,1,0:T(8,128)S(1)} collective-permute-done((f32[16,8,128]{2,1,0:T(8,128)S(1)}, f32[16,8,128]{2,1,0:T(8,128)S(1)}, u32[]{:S(2)}, u32[]{:S(2)}) %collective-permute-start.5) | collective-permute-done | bytes 65568 | tf_op jit(solution)/shard_map/ppermute | solution.py:12
  47.0 0.1 broadcast_select_fusion.3
  47.1 6.5 %all_to_all.10 = f32[16,8,128]{2,1,0:T(8,128)S(1)} all-to-all(f32[16,8,128]{2,1,0:T(8,128)S(1)} %broadcast_select_fusion.3), channel_id=1, replica_groups=mesh['row'=4,'col'=8] {'row'}, dimensions={0} | all-to-all | bytes 131072 | tf_op jit(solution)/shard_map/all_to_all | solution.py:55
  53.6 0.9 %fusion.10 = f32[16,8,128]{2,1,0:T(8,128)S(1)} fusion(f32[16,8,128]{2,1,0:T(8,128)S(1)} %all_to_all.10, bf16[16,128,128]{2,1,0:T(8,128)(2,1)S(1)} %copy-done.1), kind=kOutput, calls=%fused_computation.28 | convolution fusion | flops 25165824 | bytes 655360 | tf_op jit(solution)/shard_map/asz,ayz->asy/dot_general | solution.py:56
  54.5 1.0 %fusion = f32[8,256,128]{1,2,0:T(8,128)S(1)} fusion(f32[16,8,128]{2,1,0:T(8,128)S(1)} %fusion.10, f32[16,256]{1,0:T(8,128)S(1)} %copy-done.3), kind=kOutput, calls=%fused_computation.1 | convolution fusion | flops 50593792 | bytes 1130496 | tf_op jit(solution)/shard_map/ax,asy->sxy/dot_general | solution.py:57
  55.5 1.3 %copy.7 = f32[8,256,128]{2,1,0:T(8,128)} copy(f32[8,256,128]{1,2,0:T(8,128)S(1)} %fusion) | data formatting | bytes 2097152
  (14 shorter events, 0.1 us)
Async XLA Ops:
  0.6 1.2 %copy-start = (f32[8,256,128]{2,1,0:T(8,128)S(1)}, f32[8,256,128]{2,1,0:T(8,128)}, u32[]{:S(2)}) copy-start(f32[8,256,128]{2,1,0:T(8,128)} %param.5) | copy-start | bytes 3145732
  0.6 2.5 %copy-start.1 = (bf16[16,128,128]{2,1,0:T(8,128)(2,1)S(1)}, bf16[16,128,128]{2,1,0:T(8,128)(2,1)}, u32[]{:S(2)}) copy-start(bf16[16,128,128]{2,1,0:T(8,128)(2,1)} %param.7) | copy-start | bytes 1572868
  4.3 8.4 %all-to-all-start = ((f32[16,8,128]{2,1,0:T(8,128)}), f32[16,8,128]{2,1,0:T(8,128)S(1)}, u32[]{:S(2)}, u32[]{:S(2)}) async-start(f32[16,8,128]{2,1,0:T(8,128)} %fusion.2), calls=%async_computation | async-start | bytes 131072 | tf_op jit(solution)/shard_map/all_to_all | solution.py:47
  8.6 0.7 %copy-start.5 = (s32[16]{0:T(128)S(1)}, s32[16]{0:T(128)}, u32[]{:S(2)}) copy-start(s32[16]{0:T(128)} %param.8) | copy-start | bytes 196
  12.7 7.2 %collective-permute-start = (f32[16,8,128]{2,1,0:T(8,128)S(1)}, f32[16,8,128]{2,1,0:T(8,128)S(1)}, u32[]{:S(2)}, u32[]{:S(2)}) collective-permute-start(f32[16,8,128]{2,1,0:T(8,128)S(1)} %all-to-all-done), channel_id=1, source_target_pairs={{0,1},{1,2},{2,3},{3,4},{4,5},{5,6},{6,7},{7,0},{8,9},{9,10},{10,1... | collective-permute-start | bytes 196616 | tf_op jit(solution)/shard_map/ppermute | solution.py:12
  20.1 6.7 %collective-permute-start.1 = (f32[16,8,128]{2,1,0:T(8,128)S(1)}, f32[16,8,128]{2,1,0:T(8,128)S(1)}, u32[]{:S(2)}, u32[]{:S(2)}) collective-permute-start(f32[16,8,128]{2,1,0:T(8,128)S(1)} %broadcast_select_fusion), channel_id=1, source_target_pairs={{0,2},{1,3},{2,4},{3,5},{4,6},{5,7},{6,0},{7,1},{8,10},{9,11},{10,... | collective-permute-start | bytes 196616 | tf_op jit(solution)/shard_map/ppermute | solution.py:12
  26.9 5.2 %collective-permute-start.2 = (f32[16,8,128]{2,1,0:T(8,128)S(1)}, f32[16,8,128]{2,1,0:T(8,128)S(1)}, u32[]{:S(2)}, u32[]{:S(2)}) collective-permute-start(f32[16,8,128]{2,1,0:T(8,128)S(1)} %broadcast_select_fusion.2), channel_id=1, source_target_pairs={{0,4},{1,5},{2,6},{3,7},{4,0},{5,1},{6,2},{7,3},{8,12},{9,13},{10,... | collective-permute-start | bytes 196616 | tf_op jit(solution)/shard_map/ppermute | solution.py:12
  32.2 0.7 %copy-start.4 = (f32[4,8,128]{2,1,0:T(8,128)S(1)}, f32[4,8,128]{2,1,0:T(8,128)}, u32[]{:S(2)}) copy-start(f32[4,8,128]{2,1,0:T(8,128)} %param.9) | copy-start | bytes 49156
  32.9 4.3 %copy-start.2 = (f32[4,8,128]{2,1,0:T(8,128)}, f32[4,8,128]{2,1,0:T(8,128)S(1)}, u32[]{:S(2)}) copy-start(f32[4,8,128]{2,1,0:T(8,128)S(1)} %sub.8) | copy-start | bytes 49156
  32.9 4.3 %collective-permute-start.3 = (f32[16,8,128]{2,1,0:T(8,128)S(1)}, f32[16,8,128]{2,1,0:T(8,128)S(1)}, u32[]{:S(2)}, u32[]{:S(2)}) collective-permute-start(f32[16,8,128]{2,1,0:T(8,128)S(1)} %bitcast.15), channel_id=1, source_target_pairs={{0,7},{1,0},{2,1},{3,2},{4,3},{5,4},{6,5},{7,6},{8,15},{9,8},{10,9... | collective-permute-start | bytes 196616 | tf_op jit(solution)/shard_map/ppermute | solution.py:12
  37.3 4.3 %collective-permute-start.4 = (f32[16,8,128]{2,1,0:T(8,128)S(1)}, f32[16,8,128]{2,1,0:T(8,128)S(1)}, u32[]{:S(2)}, u32[]{:S(2)}) collective-permute-start(f32[16,8,128]{2,1,0:T(8,128)S(1)} %bitcast_select_fusion), channel_id=1, source_target_pairs={{0,6},{1,7},{2,0},{3,1},{4,2},{5,3},{6,4},{7,5},{8,14},{9,15},{10,... | collective-permute-start | bytes 196616 | tf_op jit(solution)/shard_map/ppermute | solution.py:12
  41.8 5.2 %collective-permute-start.5 = (f32[16,8,128]{2,1,0:T(8,128)S(1)}, f32[16,8,128]{2,1,0:T(8,128)S(1)}, u32[]{:S(2)}, u32[]{:S(2)}) collective-permute-start(f32[16,8,128]{2,1,0:T(8,128)S(1)} %broadcast_select_fusion.1), channel_id=1, source_target_pairs={{0,4},{1,5},{2,6},{3,7},{4,0},{5,1},{6,2},{7,3},{8,12},{9,13},{10,... | collective-permute-start | bytes 196616 | tf_op jit(solution)/shard_map/ppermute | solution.py:12
  53.6 0.9 %copy-start.3 = (f32[16,256]{1,0:T(8,128)S(1)}, f32[16,256]{1,0:T(8,128)}, u32[]{:S(2)}) copy-start(f32[16,256]{1,0:T(8,128)} %param.6) | copy-start | bytes 49156
where the time goes:
time: 57.3 us; the launch traced here: 56.8 us
  waiting for transfers between devices  33.8 us (59%)
  starting transfers between devices  6.75 us (12%)
  blocking collectives  6.49 us (11%)
  matrix products  4.44 us (8%)
  local copies, waits for them, and re-layouts  4.05 us (7%)
  between operations  0.76 us (1%)
    ppermute x6, waiting for transfers between devices, from_behind(): return lax.ppermute(value, axis, pairs)  30.5 us
    all_to_all x1, blocking collectives, on_device(): lax.all_to_all(shifted, 'row', split_axis=0, concat_axis=0, tiled=True)  6.49 us
    all_to_all x1, starting transfers between devices, on_device(): lax.all_to_all(outgoing, 'row', split_axis=0, concat_axis=0, tiled=True)  4.26 us
    unnamed x13, local copies, waits for them, and re-layouts  3.88 us
    all_to_all x1, waiting for transfers between devices, on_device(): lax.all_to_all(outgoing, 'row', split_axis=0, concat_axis=0, tiled=True)  3.28 us
    ppermute x6, starting transfers between devices, from_behind(): return lax.ppermute(value, axis, pairs)  2.48 us
    dot_general x1, matrix products, on_device(): jnp.einsum('ax,sxy->asy', ray_weights, volume, precision=highest) * factor  1.32 us
    dot_general x1, matrix products, on_device(): outgoing = jnp.einsum('asy,ayz->asz', tilesum, shear, precision=highest)  1.17 us
  transfers between devices with their start and end apart: 7, of which 7 were waited for; matrix products, arithmetic and copies ran while one was open for 0% of the time, Pallas kernels for 0%

commit v1 on v0

v1 whole, which is shorter than its diff:
```python
import functools
import math

import jax
import jax.numpy as jnp
from jax import lax
from jax.experimental import pallas as pl
from jax.experimental.pallas import tpu as pltpu
from jax.sharding import PartitionSpec as P

MESH = pl.DeviceIdType.MESH
UNROLL_UP_TO = 64


def split(value):
    high = value.astype(jnp.bfloat16)
    return high, (value - high.astype(jnp.float32)).astype(jnp.bfloat16)


def each(count, body):
    if count <= UNROLL_UP_TO:
        for step in range(count):
            body(step)
    else:
        lax.fori_loop(0, count, lambda step, _: (body(step), 0)[1], 0)


def bytes_of(ref, blocks, sem):
    part = ref.at[pl.ds(0, blocks)]
    return pltpu.make_async_copy(part, part, sem)


def kernel(
    rows, cols, factor,
    volume_ref, weights_ref, shear_ref, offsets_ref, measured_ref,
    residual_ref, gradient_ref,
    slab, shear, tiles, sends, landed, measure_out, measure_in, resid, pulls, pulled, resid_in,
    slab_sem, shear_sem, out_sem, in_sem, back_out_sem, back_in_sem, m_out_sem, m_in_sem, r_out_sem, r_in_sem,
):
    slices = volume_ref.shape[0]
    angles = weights_ref.shape[0]
    unit = landed.shape[1]
    pieces = slices // unit
    count = rows * cols
    row, col = lax.axis_index("row"), lax.axis_index("col")
    me = row * cols + col

    def peer(step):
        other = lax.rem(me + step + 1, count)
        return other, (other // cols, lax.rem(other, cols))

    def mate(step):
        other = lax.rem(col + step + 1, cols)
        return other, (row, other)

    volume_copies = []
    for s in range(slices):
        copy = pltpu.make_async_copy(volume_ref.at[s], slab.at[s], slab_sem.at[s])
        copy.start()
        volume_copies.append(copy)
    shear_copy = pltpu.make_async_copy(shear_ref, shear, shear_sem)
    shear_copy.start()

    barrier = pltpu.get_barrier_semaphore()
    each(count - 1, lambda step: pl.semaphore_signal(barrier, inc=1, device_id=peer(step)[1], device_id_type=MESH))

    for m in range(cols):
        angle, first = (m * unit) // slices, (m * unit) % slices
        measure_out[m] = measured_ref[angle, first:first + unit, :]

    weights = weights_ref[...] * factor
    w_high, w_low = split(weights)
    w_both = jnp.concatenate([w_high, w_low], axis=0)
    for s in range(slices):
        volume_copies[s].wait()
        v_high, v_low = split(slab[s])
        first = jnp.dot(w_both, v_high, preferred_element_type=jnp.float32)
        second = jnp.dot(w_high, v_low, preferred_element_type=jnp.float32)
        tiles[pl.ds(s, angles, stride=slices), :] = first[:angles] + first[angles:] + second
    shear_copy.wait()
    for a in range(angles):
        t_high, t_low = split(tiles[a * slices:(a + 1) * slices, :])
        both = jnp.dot(jnp.concatenate([t_high, t_low], axis=0), shear[a], preferred_element_type=jnp.float32)
        done = both[:slices] + both[slices:]
        for h in range(pieces):
            sends[a * pieces + h] = done[h * unit:(h + 1) * unit]

    pl.semaphore_wait(barrier, count - 1)

    def send_measured(step):
        other, device = mate(step)
        pltpu.make_async_remote_copy(
            src_ref=measure_out.at[other], dst_ref=measure_in.at[col], send_sem=m_out_sem, recv_sem=m_in_sem,
            device_id=device, device_id_type=MESH).start()

    def send_tile(step):
        other, device = peer(step)
        pltpu.make_async_remote_copy(
            src_ref=sends.at[other], dst_ref=landed.at[me], send_sem=out_sem, recv_sem=in_sem,
            device_id=device, device_id_type=MESH).start()

    each(cols - 1, send_measured)
    each(count - 1, send_tile)
    landed[me] = sends[me]
    measure_in[col] = measure_out[col]
    w_columns = jnp.concatenate([weights, weights - w_high.astype(jnp.float32), weights], axis=0).T.astype(jnp.bfloat16)
    offset = offsets_ref[me // pieces]
    bytes_of(measure_in, cols - 1, m_in_sem).wait()
    bytes_of(landed, count - 1, in_sem).wait()

    for c in range(cols):
        total = landed[c]
        for r in range(1, rows):
            total = total + landed[r * cols + lax.rem((cols - offset) * r + c, cols)]
        resid[c] = total - measure_in[c]

    for r in range(rows):
        for c in range(cols):
            pulls[r * cols + c] = resid[lax.rem(offset * r + c, cols)]

    def send_pull(step):
        other, device = peer(step)
        pltpu.make_async_remote_copy(
            src_ref=pulls.at[other], dst_ref=pulled.at[me], send_sem=back_out_sem, recv_sem=back_in_sem,
            device_id=device, device_id_type=MESH).start()

    def send_resid(step):
        other, device = mate(step)
        pltpu.make_async_remote_copy(
            src_ref=resid.at[other], dst_ref=resid_in.at[col], send_sem=r_out_sem, recv_sem=r_in_sem,
            device_id=device, device_id_type=MESH).start()

    each(count - 1, send_pull)
    each(cols - 1, send_resid)
    pulled[me] = pulls[me]
    resid_in[col] = resid[col]
    bytes_of(pulled, count - 1, back_in_sem).wait()

    for a in range(angles):
        value = jnp.concatenate([pulled[a * pieces + h] for h in range(pieces)], axis=0)
        p_high, p_low = split(value)
        both = lax.dot_general(
            jnp.concatenate([p_high, p_low], axis=0), shear[a], (((1,), (1,)), ((), ())),
            preferred_element_type=jnp.float32)
        tiles[a * slices:(a + 1) * slices, :] = both[:slices] + both[slices:]
    for s in range(slices):
        g_high, g_low = split(tiles[pl.ds(s, angles, stride=slices), :])
        gradient_ref[s] = jnp.dot(
            w_columns, jnp.concatenate([g_high, g_high, g_low], axis=0), preferred_element_type=jnp.float32)

    bytes_of(resid_in, cols - 1, r_in_sem).wait()
    for m in range(cols):
        angle, first = (m * unit) // slices, (m * unit) % slices
        residual_ref[angle, first:first + unit, :] = resid_in[m]
    bytes_of(measure_out, cols - 1, m_out_sem).wait()
    bytes_of(sends, count - 1, out_sem).wait()
    bytes_of(pulls, count - 1, back_out_sem).wait()
    bytes_of(resid, cols - 1, r_out_sem).wait()


def on_device(volume, ray_weights, shear_weights, shear_offsets, measured):
    rows, cols = lax.axis_size("row"), lax.axis_size("col")
    slices, slab_rows, width = volume.shape
    angles = ray_weights.shape[0]
    unit = measured.shape[0] * slices // cols
    count = rows * cols
    f32 = jnp.float32
    blocks = pltpu.VMEM((count, unit, width), f32)
    few = pltpu.VMEM((cols, unit, width), f32)
    dma = pltpu.SemaphoreType.DMA
    vmem = pl.BlockSpec(memory_space=pltpu.VMEM)
    return pl.pallas_call(
        functools.partial(kernel, rows, cols, 1.0 / math.sqrt(slab_rows * rows)),
        out_shape=(jax.ShapeDtypeStruct(measured.shape, f32), jax.ShapeDtypeStruct(volume.shape, f32)),
        in_specs=[
            pl.BlockSpec(memory_space=pl.ANY), vmem, pl.BlockSpec(memory_space=pl.ANY),
            pl.BlockSpec(memory_space=pltpu.SMEM), vmem],
        out_specs=(vmem, vmem),
        scratch_shapes=[
            pltpu.VMEM(volume.shape, f32),
            pltpu.VMEM(shear_weights.shape, shear_weights.dtype),
            pltpu.VMEM((angles * slices, width), f32),
            blocks, blocks, few, few, few, blocks, blocks, few,
            dma((slices,)), dma, dma, dma, dma, dma, dma, dma, dma, dma,
        ],
        compiler_params=pltpu.CompilerParams(collective_id=0, has_side_effects=True),
        name="project",
    )(volume, ray_weights, shear_weights, shear_offsets, measured)


def solution(mesh):
    placed = (P(None, "row", "col"), P(None, "row"), P(), P(), P("row", None, "col"))
    return jax.shard_map(
        on_device,
        mesh=mesh,
        in_specs=placed,
        out_specs=(P("row", None, "col"), P(None, "row", "col")),
        check_vma=False,
    )
```

time: 57.3 us -> 24.2 us (0.42)
  waiting for transfers between devices: 33.8 us -> 0 us
  Pallas kernels: 0 us -> 19.6 us
  starting transfers between devices: 6.75 us -> 0 us
  blocking collectives: 6.49 us -> 0 us
  matrix products: 4.44 us -> 0 us
    ppermute x6 -> x0, waiting for transfers between devices: 30.5 us -> none  [from_behind(): return lax.ppermute(value, axis, pairs)]
    pallas_call x0 -> x1, Pallas kernels: none -> 19.6 us  [on_device(): pl.pallas_call(functools.partial(kernel, rows, cols, 1.0 / math.sqrt(slab...]
    all_to_all x1 -> x0, blocking collectives: 6.49 us -> none  [on_device(): lax.all_to_all(shifted, 'row', split_axis=0, concat_axis=0, tiled=True)]
    dot_general x4 -> x0, matrix products: 4.44 us -> none  [the longest x1 1.32 us: on_device(): jnp.einsum('ax,sxy->asy', ray_weights, volume, precision=highest) * factor]
    all_to_all x1 -> x0, starting transfers between devices: 4.26 us -> none  [on_device(): lax.all_to_all(outgoing, 'row', split_axis=0, concat_axis=0, tiled=True)]
    all_to_all x1 -> x0, waiting for transfers between devices: 3.28 us -> none  [on_device(): lax.all_to_all(outgoing, 'row', split_axis=0, concat_axis=0, tiled=True)]
    ppermute x6 -> x0, starting transfers between devices: 2.48 us -> none  [from_behind(): return lax.ppermute(value, axis, pairs)]
    unnamed x13 -> x2, local copies, waits for them, and re-layouts: 3.88 us -> 3.59 us
  transfers between devices with their start and end apart: 7 -> 0, of which waited for: 7 -> 0; matrix products, arithmetic and copies ran while one was open for 0% -> 0% of each run, Pallas kernels for 0% -> 0%
where the time goes in v1:
time: 24.2 us; the launch traced here: 23.8 us
  Pallas kernels  19.6 us (81%)
  local copies, waits for them, and re-layouts  3.59 us (15%)
  between operations  0.64 us (3%)
    pallas_call x1, Pallas kernels, on_device(): pl.pallas_call(functools.partial(kernel, rows, cols, 1.0 / math.sqrt(slab...  19.6 us
    unnamed x2, local copies, waits for them, and re-layouts  3.59 us

profile of v1, /device:TPU:0, one launch (start us, length us, event | category | flops | bytes accessed | tf_op | source)
XLA Modules:
  0.0 23.8 jit_solution(15164121952336521037)
XLA Ops:
  0.6 19.6 %project.1 = (f32[4,8,128]{2,1,0:T(8,128)}, f32[8,256,128]{2,1,0:T(8,128)}) custom-call(f32[8,256,128]{2,1,0:T(8,128)} %volume_ref.1, f32[16,256]{1,0:T(8,128)} %weights_ref.1, bf16[16,128,128]{2,1,0:T(8,128)(2,1)} %shear_ref.1, s32[16]{0:T(128)} %offsets_ref.1, f32[4,8,128]{2,1,0:T(8,128)} %measured_ref.1), custom_call_target="tpu_custom_call" | custom-call | tf_op jit(solution)/shard_map/project/pallas_call | solution.py:172
  20.2 1.3 %copy.9 = f32[4,8,128]{2,1,0:T(8,128)} copy(f32[4,8,128]{2,1,0:T(8,128)} %get-tuple-element.4) | data formatting | bytes 32768
  21.5 2.3 %copy.10 = f32[8,256,128]{2,1,0:T(8,128)} copy(f32[8,256,128]{2,1,0:T(8,128)} %get-tuple-element.5) | data formatting | bytes 2097152

commit v2 on v1

v2 whole, which is shorter than its diff:
```python
import functools
import math

import jax
import jax.numpy as jnp
from jax import lax
from jax.experimental import pallas as pl
from jax.experimental.pallas import tpu as pltpu
from jax.sharding import PartitionSpec as P

MESH = pl.DeviceIdType.MESH
UNROLL_UP_TO = 64
KERNEL_VMEM = 24 * 1024 * 1024


def split(value):
    high = value.astype(jnp.bfloat16)
    return high, (value - high.astype(jnp.float32)).astype(jnp.bfloat16)


def each(count, body):
    if count <= UNROLL_UP_TO:
        for step in range(count):
            body(step)
    else:
        lax.fori_loop(0, count, lambda step, _: (body(step), 0)[1], 0)


def bytes_of(ref, blocks, sem):
    part = ref.at[pl.ds(0, blocks)]
    return pltpu.make_async_copy(part, part, sem)


def exchange(
    rows, cols, factor,
    volume_ref, weights_ref, shear_ref, offsets_ref, measured_ref,
    columns_ref, spread_ref, residual_ref,
    slab, weights_in, shear, offsets, measured, sums, tiles, landed, measure_in, resid, pulls, pulled, resid_in,
    slab_sem, local_sem, out_sem, in_sem, back_out_sem, back_in_sem, m_out_sem, m_in_sem, r_out_sem, r_in_sem,
):
    slices = volume_ref.shape[0]
    angles = weights_ref.shape[0]
    owned = measured_ref.shape[0]
    base = (cols - owned) // 2
    count = rows * cols
    row, col = lax.axis_index("row"), lax.axis_index("col")
    me = row * cols + col
    at_home = jnp.logical_and(col >= base, col < base + owned)
    away = jnp.logical_not(at_home)
    mine = row * owned + lax.clamp(0, col - base, owned - 1)

    def home(angle):
        return angle // owned, base + lax.rem(angle, owned)

    def peer(step):
        other = lax.rem(me + step + 1, count)
        return other, (other // cols, lax.rem(other, cols))

    def signal(device):
        pl.semaphore_signal(barrier, inc=1, device_id=device, device_id_type=MESH)

    weights_copy = pltpu.make_async_copy(weights_ref, weights_in, local_sem.at[0])
    weights_copy.start()
    volume_copies = []
    for s in range(slices):
        copy = pltpu.make_async_copy(volume_ref.at[s], slab.at[s], slab_sem.at[s])
        copy.start()
        volume_copies.append(copy)
    shear_copy = pltpu.make_async_copy(shear_ref, shear, local_sem.at[1])
    shear_copy.start()
    measured_copy = pltpu.make_async_copy(measured_ref, measured, local_sem.at[2])
    measured_copy.start()
    offsets_copy = pltpu.make_async_copy(offsets_ref, offsets, local_sem.at[3])
    offsets_copy.start()

    barrier = pltpu.get_barrier_semaphore()

    @pl.when(at_home)
    def _():
        each(count - 1, lambda step: signal(peer(step)[1]))

    @pl.when(away)
    def _():
        each(angles, lambda angle: signal(home(angle)))

    weights_copy.wait()
    weights = weights_in[...] * factor
    w_high, w_low = split(weights)
    w_both = jnp.concatenate([w_high, w_low], axis=0)
    for s in range(slices):
        volume_copies[s].wait()
        v_high, v_low = split(slab[s])
        first = jnp.dot(w_both, v_high, preferred_element_type=jnp.float32)
        second = jnp.dot(w_high, v_low, preferred_element_type=jnp.float32)
        sums[pl.ds(s, angles, stride=slices), :] = first[:angles] + first[angles:] + second
    shear_copy.wait()
    for a in range(angles):
        t_high, t_low = split(sums[a * slices:(a + 1) * slices, :])
        both = jnp.dot(jnp.concatenate([t_high, t_low], axis=0), shear[a], preferred_element_type=jnp.float32)
        tiles[a] = both[:slices] + both[slices:]
    measured_copy.wait()
    offsets_copy.wait()

    @pl.when(at_home)
    def _():
        pl.semaphore_wait(barrier, count - 1)

    @pl.when(away)
    def _():
        pl.semaphore_wait(barrier, angles)

    def send(source, target, send_sem, recv_sem, device):
        pltpu.make_async_remote_copy(
            src_ref=source, dst_ref=target, send_sem=send_sem, recv_sem=recv_sem,
            device_id=device, device_id_type=MESH).start()

    def send_measured(step):
        place = lax.rem(lax.select(at_home, col - base + 1, 0) + step, owned)
        send(measured.at[place], measure_in.at[col], m_out_sem, m_in_sem, (row, base + place))

    def send_tile(step):
        angle = lax.rem(lax.select(at_home, mine + 1, row * owned) + step, angles)
        send(tiles.at[angle], landed.at[me], out_sem, in_sem, home(angle))

    each(angles - 1, send_tile)

    @pl.when(away)
    def _():
        send_tile(angles - 1)

    each(owned - 1, send_measured)

    @pl.when(away)
    def _():
        send_measured(owned - 1)

    columns_ref[...] = jnp.concatenate(
        [weights, weights - w_high.astype(jnp.float32), weights], axis=0).T.astype(jnp.bfloat16)

    @pl.when(at_home)
    def _():
        landed[me] = tiles[mine]
        measure_in[col] = measured[col - base]
        offset = offsets[mine]
        bytes_of(measure_in, cols - 1, m_in_sem).wait()
        bytes_of(landed, count - 1, in_sem).wait()
        for c in range(cols):
            total = landed[c]
            for r in range(1, rows):
                total = total + landed[r * cols + lax.rem((cols - offset) * r + c, cols)]
            resid[c] = total - measure_in[c]
        for r in range(rows):
            for c in range(cols):
                pulls[r * cols + c] = resid[lax.rem(offset * r + c, cols)]

        def send_pull(step):
            other, device = peer(step)
            send(pulls.at[other], pulled.at[mine], back_out_sem, back_in_sem, device)

        def send_resid(step):
            other = lax.rem(col + step + 1, cols)
            send(resid.at[other], resid_in.at[col - base], r_out_sem, r_in_sem, (row, other))

        each(count - 1, send_pull)
        each(cols - 1, send_resid)
        pulled[mine] = pulls[me]
        resid_in[col - base] = resid[col]
        bytes_of(pulled, angles - 1, back_in_sem).wait()

    @pl.when(away)
    def _():
        bytes_of(pulled, angles, back_in_sem).wait()

    for a in range(angles):
        p_high, p_low = split(pulled[a])
        both = lax.dot_general(
            jnp.concatenate([p_high, p_low], axis=0), shear[a], (((1,), (1,)), ((), ())),
            preferred_element_type=jnp.float32)
        sums[a * slices:(a + 1) * slices, :] = both[:slices] + both[slices:]
    for s in range(slices):
        g_high, g_low = split(sums[pl.ds(s, angles, stride=slices), :])
        spread_ref[s] = jnp.concatenate([g_high, g_high, g_low], axis=0)

    @pl.when(at_home)
    def _():
        bytes_of(resid_in, owned - 1, r_in_sem).wait()
        bytes_of(tiles, angles - 1, out_sem).wait()
        bytes_of(measured, owned - 1, m_out_sem).wait()
        bytes_of(pulls, count - 1, back_out_sem).wait()
        bytes_of(resid, cols - 1, r_out_sem).wait()

    @pl.when(away)
    def _():
        bytes_of(resid_in, owned, r_in_sem).wait()
        bytes_of(tiles, angles, out_sem).wait()
        bytes_of(measured, owned, m_out_sem).wait()

    residual_ref[...] = resid_in[...]


def finish(columns_ref, spread_ref, resid_ref, residual_ref, gradient_ref, stage, stage_sem, resid_sem):
    copies = [pltpu.make_async_copy(resid_ref, residual_ref, resid_sem)]
    copies[0].start()
    for s in range(spread_ref.shape[0]):
        stage[s] = jnp.dot(columns_ref[...], spread_ref[s], preferred_element_type=jnp.float32)
        copy = pltpu.make_async_copy(stage.at[s], gradient_ref.at[s], stage_sem.at[s])
        copy.start()
        copies.append(copy)
    for copy in copies:
        copy.wait()


def on_device(volume, ray_weights, shear_weights, shear_offsets, measured):
    rows, cols = lax.axis_size("row"), lax.axis_size("col")
    slices, slab_rows, width = volume.shape
    angles = ray_weights.shape[0]
    owned = measured.shape[0]
    count = rows * cols
    f32, bf16 = jnp.float32, jnp.bfloat16
    dma = pltpu.SemaphoreType.DMA
    vmem = pl.BlockSpec(memory_space=pltpu.VMEM)
    hbm = pl.BlockSpec(memory_space=pltpu.HBM)

    def blocks(number):
        return pltpu.VMEM((number, slices, width), f32)

    columns, spread, resid = pl.pallas_call(
        functools.partial(exchange, rows, cols, 1.0 / math.sqrt(slab_rows * rows)),
        out_shape=(
            jax.ShapeDtypeStruct((slab_rows, 3 * angles), bf16),
            jax.ShapeDtypeStruct((slices, 3 * angles, width), bf16),
            jax.ShapeDtypeStruct(measured.shape, f32)),
        in_specs=[hbm] * 5,
        out_specs=(vmem, vmem, vmem),
        scratch_shapes=[
            pltpu.VMEM(volume.shape, f32),
            pltpu.VMEM(ray_weights.shape, f32),
            pltpu.VMEM(shear_weights.shape, shear_weights.dtype),
            pltpu.SMEM(shear_offsets.shape, jnp.int32),
            blocks(owned),
            pltpu.VMEM((angles * slices, width), f32),
            blocks(angles), blocks(count), blocks(cols), blocks(cols), blocks(count), blocks(angles), blocks(owned),
            dma((slices,)), dma((4,)), dma, dma, dma, dma, dma, dma, dma, dma,
        ],
        compiler_params=pltpu.CompilerParams(collective_id=0, has_side_effects=True, vmem_limit_bytes=KERNEL_VMEM),
        name="exchange",
    )(*(pltpu.with_memory_space_constraint(value, pltpu.HBM)
        for value in (volume, ray_weights, shear_weights, shear_offsets, measured)))
    return pl.pallas_call(
        finish,
        out_shape=(jax.ShapeDtypeStruct(measured.shape, f32), jax.ShapeDtypeStruct(volume.shape, f32)),
        in_specs=[vmem] * 3,
        out_specs=(hbm, hbm),
        scratch_shapes=[pltpu.VMEM(volume.shape, f32), dma((slices,)), dma],
        compiler_params=pltpu.CompilerParams(vmem_limit_bytes=KERNEL_VMEM),
        name="finish",
    )(columns, spread, resid)


def solution(mesh):
    placed = (P(None, "row", "col"), P(None, "row"), P(), P(), P("row", None, "col"))
    return jax.shard_map(
        on_device,
        mesh=mesh,
        in_specs=placed,
        out_specs=(P("row", None, "col"), P(None, "row", "col")),
        check_vma=False,
    )
```

time: 24.2 us -> 18.1 us (0.75)
  local copies, waits for them, and re-layouts: 3.59 us -> 0 us
  Pallas kernels: 19.6 us -> 17.3 us
    unnamed x2 -> x0, local copies, waits for them, and re-layouts: 3.59 us -> none
    pallas_call x1 -> x2, Pallas kernels: 19.6 us -> 17.3 us  [the longest x1 16.1 us: on_device(): pl.pallas_call(functools.partial(exchange, rows, cols, 1.0 / math.sqrt(sl...]
where the time goes in v2:
time: 18.1 us; the launch traced here: 17.9 us
  Pallas kernels  17.3 us (96%)
  between operations  0.64 us (4%)
    pallas_call x1, Pallas kernels, on_device(): pl.pallas_call(functools.partial(exchange, rows, cols, 1.0 / math.sqrt(sl...  16.1 us
    pallas_call x1, Pallas kernels, on_device(): pl.pallas_call(finish, out_shape=(jax.ShapeDtypeStruct(measured.shape, f3...  1.2 us

profile of v2, /device:TPU:0, one launch (start us, length us, event | category | flops | bytes accessed | tf_op | source)
XLA Modules:
  0.0 17.9 jit_solution(3681003296977938464)
XLA Ops:
  0.6 16.1 %exchange.1 = (bf16[256,48]{1,0:T(8,128)(2,1)S(1)}, bf16[8,48,128]{2,1,0:T(8,128)(2,1)S(1)}, f32[4,8,128]{2,1,0:T(8,128)S(1)}) custom-call(f32[8,256,128]{2,1,0:T(8,128)} %volume_ref.1, f32[16,256]{1,0:T(8,128)} %weights_ref.1, bf16[16,128,128]{2,1,0:T(8,128)(2,1)} %shear_ref.1, s32[16]{0:T(128)} %offsets_ref.1, f32[4,8,128]{2,1,0:T(8,128)} %measured_ref.1), custom_call_target="tpu_custom_call" | custom-call | tf_op jit(solution)/shard_map/exchange/pallas_call | solution.py:227
  16.7 1.2 %finish.1 = (f32[4,8,128]{2,1,0:T(8,128)}, f32[8,256,128]{2,1,0:T(8,128)}) custom-call(bf16[256,48]{1,0:T(8,128)(2,1)S(1)} %get-tuple-element.5.columns_ref, bf16[8,48,128]{2,1,0:T(8,128)(2,1)S(1)} %get-tuple-element.6.spread_ref, f32[4,8,128]{2,1,0:T(8,128)S(1)} %get-tuple-element.7.resid_ref), custom_call_target="tpu_custom_call" | custom-call | tf_op jit(solution)/shard_map/finish/pallas_call | solution.py:249

commit v3 on v2

--- a/solution.py
+++ b/solution.py
@@ -24,6 +24,23 @@
             body(step)
     else:
         lax.fori_loop(0, count, lambda step, _: (body(step), 0)[1], 0)
+
+
+def flip(index, step, size):
+    if size & (size - 1):
+        return lax.rem(index + step, size)
+    bit = 1
+    while bit < size:
+        if step & bit:
+            index = index + bit - 2 * bit * lax.rem(index // bit, 2)
+        bit *= 2
+    return index
+
+
+def far_first(size):
+    quarter = max(size // 4, 1)
+    place = {2: 0, 3: 1, 1: 2, 0: 3}
+    return sorted(range(size), key=lambda step: (place.get(step // quarter, 2), -step))
 
 
 def bytes_of(ref, blocks, sem):
@@ -52,12 +69,27 @@
     def home(angle):
         return angle // owned, base + lax.rem(angle, owned)
 
+    unrolled = count <= UNROLL_UP_TO
+    other_rows = [flip(row, step, rows) for step in reversed(range(rows))] if unrolled else None
+    other_cols = [flip(col, step, cols) for step in far_first(cols)] if unrolled else None
+    near = lax.clamp(0, col - base, owned - 1)
+    other_places = [flip(near, step, owned) for step in far_first(owned)] if unrolled else None
+
     def peer(step):
+        if unrolled:
+            target = other_rows[step % rows], other_cols[step // rows]
+            return target[0] * cols + target[1], target
         other = lax.rem(me + step + 1, count)
         return other, (other // cols, lax.rem(other, cols))
 
     def signal(device):
         pl.semaphore_signal(barrier, inc=1, device_id=device, device_id_type=MESH)
+
+    barrier = pltpu.get_barrier_semaphore()
+
+    @pl.when(at_home)
+    def _():
+        each(count - 1, lambda step: signal(peer(step)[1]))
 
     weights_copy = pltpu.make_async_copy(weights_ref, weights_in, local_sem.at[0])
     weights_copy.start()
@@ -72,12 +104,6 @@
     measured_copy.start()
     offsets_copy = pltpu.make_async_copy(offsets_ref, offsets, local_sem.at[3])
     offsets_copy.start()
-
-    barrier = pltpu.get_barrier_semaphore()
-
-    @pl.when(at_home)
-    def _():
-        each(count - 1, lambda step: signal(peer(step)[1]))
 
     @pl.when(away)
     def _():
@@ -115,24 +141,24 @@
             device_id=device, device_id_type=MESH).start()
 
     def send_measured(step):
-        place = lax.rem(lax.select(at_home, col - base + 1, 0) + step, owned)
+        place = other_places[step] if unrolled else lax.rem(lax.select(at_home, col - base + 1, 0) + step, owned)
         send(measured.at[place], measure_in.at[col], m_out_sem, m_in_sem, (row, base + place))
 
     def send_tile(step):
+        if unrolled:
+            target, place = other_rows[step % rows], other_places[step // rows]
+            send(tiles.at[target * owned + place], landed.at[me], out_sem, in_sem, (target, base + place))
+            return
         angle = lax.rem(lax.select(at_home, mine + 1, row * owned) + step, angles)
         send(tiles.at[angle], landed.at[me], out_sem, in_sem, home(angle))
 
+    each(owned - 1, send_measured)
     each(angles - 1, send_tile)
 
     @pl.when(away)
     def _():
+        send_measured(owned - 1)
         send_tile(angles - 1)
-
-    each(owned - 1, send_measured)
-
-    @pl.when(away)
-    def _():
-        send_measured(owned - 1)
 
     columns_ref[...] = jnp.concatenate(
         [weights, weights - w_high.astype(jnp.float32), weights], axis=0).T.astype(jnp.bfloat16)
@@ -158,7 +184,7 @@
             send(pulls.at[other], pulled.at[mine], back_out_sem, back_in_sem, device)
 
         def send_resid(step):
-            other = lax.rem(col + step + 1, cols)
+            other = other_cols[step] if unrolled else lax.rem(col + step + 1, cols)
             send(resid.at[other], resid_in.at[col - base], r_out_sem, r_in_sem, (row, other))
 
         each(count - 1, send_pull)

time: 18.1 us -> 17.8 us (0.983)
  Pallas kernels: 17.3 us -> 17 us
    pallas_call x1, Pallas kernels: 16.1 us -> 15.8 us  [on_device(): pl.pallas_call(functools.partial(exchange, rows, cols, 1.0 / math.sqrt(sl...]
where the time goes in v3:
time: 17.8 us; the launch traced here: 17.6 us
  Pallas kernels  17 us (96%)
  between operations  0.64 us (4%)
    pallas_call x1, Pallas kernels, on_device(): pl.pallas_call(functools.partial(exchange, rows, cols, 1.0 / math.sqrt(sl...  15.8 us
    pallas_call x1, Pallas kernels, on_device(): pl.pallas_call(finish, out_shape=(jax.ShapeDtypeStruct(measured.shape, f3...  1.2 us

profile of v3, /device:TPU:0, one launch (start us, length us, event | category | flops | bytes accessed | tf_op | source)
XLA Modules:
  0.0 17.6 jit_solution(4868094767999307611)
XLA Ops:
  0.6 15.8 %exchange.1 = (bf16[256,48]{1,0:T(8,128)(2,1)S(1)}, bf16[8,48,128]{2,1,0:T(8,128)(2,1)S(1)}, f32[4,8,128]{2,1,0:T(8,128)S(1)}) custom-call(f32[8,256,128]{2,1,0:T(8,128)} %volume_ref.1, f32[16,256]{1,0:T(8,128)} %weights_ref.1, bf16[16,128,128]{2,1,0:T(8,128)(2,1)} %shear_ref.1, s32[16]{0:T(128)} %offsets_ref.1, f32[4,8,128]{2,1,0:T(8,128)} %measured_ref.1), custom_call_target="tpu_custom_call" | custom-call | tf_op jit(solution)/shard_map/exchange/pallas_call | solution.py:253
  16.4 1.2 %finish.1 = (f32[4,8,128]{2,1,0:T(8,128)}, f32[8,256,128]{2,1,0:T(8,128)}) custom-call(bf16[256,48]{1,0:T(8,128)(2,1)S(1)} %get-tuple-element.5.columns_ref, bf16[8,48,128]{2,1,0:T(8,128)(2,1)S(1)} %get-tuple-element.6.spread_ref, f32[4,8,128]{2,1,0:T(8,128)S(1)} %get-tuple-element.7.resid_ref), custom_call_target="tpu_custom_call" | custom-call | tf_op jit(solution)/shard_map/finish/pallas_call | solution.py:275

commit v4 on v3

--- a/solution.py
+++ b/solution.py
@@ -152,8 +152,8 @@
         angle = lax.rem(lax.select(at_home, mine + 1, row * owned) + step, angles)
         send(tiles.at[angle], landed.at[me], out_sem, in_sem, home(angle))
 
+    each(angles - 1, send_tile)
     each(owned - 1, send_measured)
-    each(angles - 1, send_tile)
 
     @pl.when(away)
     def _():

time: 17.8 us -> 17.5 us (0.983)
  Pallas kernels: 17 us -> 16.8 us
    pallas_call x1, Pallas kernels: 15.8 us -> 15.6 us  [on_device(): pl.pallas_call(functools.partial(exchange, rows, cols, 1.0 / math.sqrt(sl...]
where the time goes in v4:
time: 17.5 us; the launch traced here: 17.4 us
  Pallas kernels  16.8 us (96%)
  between operations  0.64 us (4%)
    pallas_call x1, Pallas kernels, on_device(): pl.pallas_call(functools.partial(exchange, rows, cols, 1.0 / math.sqrt(sl...  15.6 us
    pallas_call x1, Pallas kernels, on_device(): pl.pallas_call(finish, out_shape=(jax.ShapeDtypeStruct(measured.shape, f3...  1.2 us

profile of v4, /device:TPU:0, one launch (start us, length us, event | category | flops | bytes accessed | tf_op | source)
XLA Modules:
  0.0 17.4 jit_solution(552246222831545616)
XLA Ops:
  0.6 15.6 %exchange.1 = (bf16[256,48]{1,0:T(8,128)(2,1)S(1)}, bf16[8,48,128]{2,1,0:T(8,128)(2,1)S(1)}, f32[4,8,128]{2,1,0:T(8,128)S(1)}) custom-call(f32[8,256,128]{2,1,0:T(8,128)} %volume_ref.1, f32[16,256]{1,0:T(8,128)} %weights_ref.1, bf16[16,128,128]{2,1,0:T(8,128)(2,1)} %shear_ref.1, s32[16]{0:T(128)} %offsets_ref.1, f32[4,8,128]{2,1,0:T(8,128)} %measured_ref.1), custom_call_target="tpu_custom_call" | custom-call | tf_op jit(solution)/shard_map/exchange/pallas_call | solution.py:253
  16.2 1.2 %finish.1 = (f32[4,8,128]{2,1,0:T(8,128)}, f32[8,256,128]{2,1,0:T(8,128)}) custom-call(bf16[256,48]{1,0:T(8,128)(2,1)S(1)} %get-tuple-element.5.columns_ref, bf16[8,48,128]{2,1,0:T(8,128)(2,1)S(1)} %get-tuple-element.6.spread_ref, f32[4,8,128]{2,1,0:T(8,128)S(1)} %get-tuple-element.7.resid_ref), custom_call_target="tpu_custom_call" | custom-call | tf_op jit(solution)/shard_map/finish/pallas_call | solution.py:275
